TPU v7x, 256 devices: a whole 4x4x8 slice. The times are simulated.
256 devices in a mesh: group: 4 (over x), dp: 16 (over z_lo, y, core), mp: 4 (over z_hi).
Axes of the slice: x: 4, y: 4, z: 8 (z_hi: 4, z_lo: 2; z = z_hi * 2 + z_lo), core: 2. Of those that a mesh axis runs over, the one named last changes fastest.
Arguments:
- block_input: bfloat16 [768, 8192], P(None, 'dp'), may hold values from -6 to 6
- parent_gate_up: bfloat16 [2, 8192, 14336], P(None, 'dp', ('group', 'mp')), may hold values from -0.0625 to 0.0625
- parent_down: bfloat16 [14336, 8192], P(('group', 'mp'), 'dp'), may hold values from -0.046875 to 0.046875
- variant_gate_up: bfloat16 [4, 2, 8192, 3584], P('group', None, 'dp', 'mp'), may hold values from -0.0625 to 0.0625
- variant_down: bfloat16 [4, 3584, 8192], P('group', 'mp', 'dp'), may hold values from -0.09375 to 0.09375
- widths: int32 [4], P('group'), may hold values from 896 to 3584, as said below
Outputs:
- grad_gate_up: float32 [4, 2, 8192, 3584], P('group', None, 'dp', 'mp')
- grad_down: float32 [4, 3584, 8192], P('group', 'mp', 'dp')
Inputs may be any that keep to these rules, and one draw needn't show every extreme that they name: Variant v uses its hidden units 0 to widths[v] - 1; one variant uses all 3584 of them and another exactly a quarter of 3584.
All inputs are finite; a program needn't handle non-finite values.
Results may differ from a plain program's by a relative error of at most 0.008.
Values may be sent and summed in bfloat16 or wider, within the bound.
No kernel may reach another device: no remote copies, remote signals or barrier semaphores. Data moves between devices by JAX's collectives and lax.ppermute only.
A program may use at most 64 MiB of HBM per device.

v0:
```python
import math
import jax
import jax.numpy as jnp
from jax import lax
from jax.sharding import PartitionSpec as P


def gated_values(pre_act, unit_mask):
    gate_value = pre_act[:, 0].astype(jnp.float32)
    up_value = pre_act[:, 1].astype(jnp.float32)
    sigmoid_gate = jax.nn.sigmoid(gate_value)
    return (gate_value * sigmoid_gate * up_value * unit_mask).astype(jnp.bfloat16)


def pre_gradient(pre_act, unit_mask, hidden_grad):
    gate_value = pre_act[:, 0].astype(jnp.float32)
    up_value = pre_act[:, 1].astype(jnp.float32)
    sigmoid_gate = jax.nn.sigmoid(gate_value)
    masked_grad = hidden_grad * unit_mask
    grad_gate = masked_grad * up_value * sigmoid_gate * (1.0 + gate_value * (1.0 - sigmoid_gate))
    grad_up = masked_grad * gate_value * sigmoid_gate
    return jnp.stack([grad_gate, grad_up], axis=1).astype(jnp.bfloat16)


def body(block_input, parent_gate_up, parent_down, variant_gate_up, variant_down, widths):
    local_gate_up = variant_gate_up[0]
    local_down = variant_down[0]
    local_units = local_down.shape[0]
    all_tokens = block_input.shape[0]
    first_unit = lax.axis_index("mp") * local_units
    unit_index = first_unit + jnp.arange(local_units, dtype=jnp.int32)
    unit_mask = (unit_index < widths[0]).astype(jnp.float32)
    parent_term = jnp.einsum(
        "td,kdf->tkf", block_input, parent_gate_up, preferred_element_type=jnp.float32
    )
    variant_term = jnp.einsum(
        "td,kdf->tkf", block_input, local_gate_up, preferred_element_type=jnp.float32
    )
    parent_rows, variant_rows = (
        lax.psum_scatter(parent_term, "dp", scatter_dimension=0, tiled=True),
        lax.psum_scatter(variant_term, "dp", scatter_dimension=0, tiled=True),
    )
    parent_pre = parent_rows.astype(jnp.bfloat16)
    variant_pre = variant_rows.astype(jnp.bfloat16)
    parent_hidden = gated_values(parent_pre, 1.0)
    parent_all, variant_all = (
        lax.all_gather(parent_hidden, "dp", axis=0, tiled=True),
        lax.all_gather(variant_pre, "dp", axis=0, tiled=True),
    )
    variant_hidden = gated_values(variant_all, unit_mask)
    teacher_part = jnp.dot(parent_all, parent_down, preferred_element_type=jnp.float32)
    student_part = jnp.dot(variant_hidden, local_down, preferred_element_type=jnp.float32)
    teacher = lax.psum(teacher_part, ("group", "mp"))
    student = lax.psum(student_part, "mp")
    loss_scale = 1.0 / math.sqrt(all_tokens)
    output_grad = ((student - teacher) * loss_scale).astype(jnp.bfloat16)
    grad_down = lax.dot_general(
        variant_hidden, output_grad, (((0,), (0,)), ((), ())), preferred_element_type=jnp.float32
    )
    hidden_part = lax.dot_general(
        output_grad, local_down, (((1,), (1,)), ((), ())), preferred_element_type=jnp.float32
    )
    hidden_full = lax.psum(hidden_part, "dp")
    grad_pre = pre_gradient(variant_all, unit_mask, hidden_full)
    grad_gate_up = jnp.einsum(
        "td,tkf->kdf", block_input, grad_pre, preferred_element_type=jnp.float32
    )
    return (grad_gate_up[None], grad_down[None])


def solution(mesh):
    in_specs = (
        P(None, "dp"),
        P(None, "dp", ("group", "mp")),
        P(("group", "mp"), "dp"),
        P("group", None, "dp", "mp"),
        P("group", "mp", "dp"),
        P("group"),
    )
    out_specs = (P("group", None, "dp", "mp"), P("group", "mp", "dp"))
    return jax.shard_map(body, mesh=mesh, in_specs=in_specs, out_specs=out_specs, check_vma=False)
```

profile of v0, /device:TPU:1, one launch (start us, length us, event | category | flops | bytes accessed | tf_op | source)
XLA Modules:
  0.0 652.1 jit_solution(2625803845936884595)
XLA Ops:
  7.2 1.4 copy-done
  8.7 5.2 fusion.45
  13.9 1.1 copy-done.1
  15.0 5.5 fusion.29
  20.5 0.0 all-gather.5.cloned.1.call-start
  20.6 66.0 %reduce-scatter.5.cloned.1.call-done = f32[48,2,896]{2,0,1:T(8,128)} async-done(((f32[768,2,896]{2,0,1:T(8,128)}), f32[48,2,896]{2,0,1:T(8,128)}) %reduce-scatter.5.cloned.1.call-update) | async-done | bytes 344080 | tf_op jit(solution)/shard_map/reduce_scatter | solution.py:40
  86.6 1.0 convert_element_type.66
  87.6 0.7 fusion.52
  88.3 0.0 all-gather.3.cloned.1.call-start
  88.4 71.3 %reduce-scatter.3.cloned.1.call-done = f32[48,2,896]{2,0,1:T(8,128)} async-done(((f32[768,2,896]{2,0,1:T(8,128)}), f32[48,2,896]{2,0,1:T(8,128)}) %reduce-scatter.3.cloned.1.call-update) | async-done | bytes 344080 | tf_op jit(solution)/shard_map/reduce_scatter | solution.py:41
  159.7 1.7 convert_element_type.60
  161.4 38.0 %all-gather.5.cloned.1.call-done = bf16[768,896]{1,0:T(8,128)(2,1)} async-done(((bf16[48,896]{1,0:T(8,128)(2,1)}), bf16[768,896]{1,0:T(8,128)(2,1)}) %all-gather.5.cloned.1.call-update) | async-done | bytes 1376272 | tf_op jit(solution)/shard_map/all_gather | solution.py:47
  199.4 3.7 fusion.57
  203.8 35.3 %all-gather.3.cloned.1.call-done = bf16[768,2,896]{2,0,1:T(8,128)(2,1)} async-done(((bf16[48,2,896]{2,0,1:T(8,128)(2,1)}), bf16[768,2,896]{2,0,1:T(8,128)(2,1)}) %all-gather.3.cloned.1.call-update) | async-done | bytes 2752528 | tf_op jit(solution)/shard_map/all_gather | solution.py:48
  239.1 4.0 fusion.31
  243.2 163.2 %all-reduce.6.cloned.1.call-done = f32[768,512]{1,0:T(8,128)} async-done(((f32[768,512]{1,0:T(8,128)}), f32[768,512]{1,0:T(8,128)}) %all-reduce.6.cloned.1.call-update) | async-done | bytes 1572880 | tf_op jit(solution)/shard_map/psum | solution.py:53
  406.4 93.0 %all-reduce.4.cloned.1.call-done = f32[768,512]{1,0:T(8,128)} async-done(((f32[768,512]{1,0:T(8,128)}), f32[768,512]{1,0:T(8,128)}) %all-reduce.4.cloned.1.call-update) | async-done | bytes 1572880 | tf_op jit(solution)/shard_map/psum | solution.py:54
  499.4 2.3 multiply_convert_fusion
  501.7 3.7 fusion.39
  505.5 4.1 convolution_bitcast_fusion
  509.6 123.6 %all-reduce.8.cloned.1.call-done = f32[768,896]{1,0:T(8,128)} async-done(((f32[768,896]{1,0:T(8,128)}), f32[768,896]{1,0:T(8,128)}) %all-reduce.8.cloned.1.call-update) | async-done | bytes 2752528 | tf_op jit(solution)/shard_map/psum | solution.py:63
  633.2 4.0 fusion.36
  637.2 3.5 fusion.26
  640.7 4.6 copy.9
  (17 shorter events, 0.3 us)
Async XLA Ops:
  7.2 1.5 copy-start
  7.2 79.4 %reduce-scatter.5.cloned.1.call-start = ((), (), s32[]{:S(2)}) async-start(), calls=%async_computation.5 | async-start | bytes 5849088 | tf_op jit(solution)/shard_map/reduce_scatter | solution.py:40
  13.9 1.1 copy-start.1
  13.9 145.8 %reduce-scatter.3.cloned.1.call-start = ((), (), s32[]{:S(2)}) async-start(), calls=%async_computation.2 | async-start | bytes 5849088 | tf_op jit(solution)/shard_map/reduce_scatter | solution.py:41
  20.5 178.9 %all-gather.5.cloned.1.call-start = ((), (), s32[]{:S(2)}) async-start(), calls=%async_computation.6 | async-start | bytes 1462272 | tf_op jit(solution)/shard_map/all_gather | solution.py:47
  88.3 150.8 %all-gather.3.cloned.1.call-start = ((), (), s32[]{:S(2)}) async-start(), calls=%async_computation.3 | async-start | bytes 2924544 | tf_op jit(solution)/shard_map/all_gather | solution.py:48
  161.3 77.8 %copy-start.2 = (bf16[1,896,512]{2,1,0:T(8,128)(2,1)S(1)}, bf16[1,896,512]{2,1,0:T(8,128)(2,1)}, u32[]{:S(2)}) copy-start(bf16[1,896,512]{2,1,0:T(8,128)(2,1)} %param.10) | copy-start | bytes 2752516
  161.4 245.1 %all-reduce.6.cloned.1.call-start = ((), (), s32[]{:S(2)}) async-start(), calls=%async_computation.7 | async-start | bytes 3145728 | tf_op jit(solution)/shard_map/psum | solution.py:53
  203.1 296.3 %all-reduce.4.cloned.1.call-start = ((), (), s32[]{:S(2)}) async-start(), calls=%async_computation.4 | async-start | bytes 3145728 | tf_op jit(solution)/shard_map/psum | solution.py:54
  243.2 390.0 %all-reduce.8.cloned.1.call-start = ((), (), s32[]{:S(2)}) async-start(), calls=%async_computation.8 | async-start | bytes 5505024 | tf_op jit(solution)/shard_map/psum | solution.py:63
Sparse Core Ops, SparseCore 0:
  14.0 72.5 reduce-scatter.4
  89.1 70.4 reduce-scatter.2
  162.1 37.2 all-gather.4
  201.6 37.4 all-gather.2
  242.2 164.1 all-reduce.5
  409.5 89.8 all-reduce.3
  505.6 127.5 all-reduce.7
where the time goes:
time: 653 us; the launch traced here: 652 us
  waiting for transfers between devices  590 us (90%)
  matrix products  29.8 us (5%)
  between operations  14.8 us (2%)
  other arithmetic  9.67 us (1%)
  local copies, waits for them, and re-layouts  7.1 us (1%)
    psum x1, waiting for transfers between devices, body(): teacher = lax.psum(teacher_part, ('group', 'mp'))  163 us
    psum x1, waiting for transfers between devices, body(): hidden_full = lax.psum(hidden_part, 'dp')  124 us
    psum x1, waiting for transfers between devices, body(): student = lax.psum(student_part, 'mp')  93 us
    reduce_scatter x1, waiting for transfers between devices, body(): lax.psum_scatter(variant_term, 'dp', scatter_dimension=0, tiled=True)  71.3 us
    reduce_scatter x1, waiting for transfers between devices, body(): lax.psum_scatter(parent_term, 'dp', scatter_dimension=0, tiled=True)  66 us
    all_gather x1, waiting for transfers between devices, body(): lax.all_gather(parent_hidden, 'dp', axis=0, tiled=True)  38 us
    all_gather x1, waiting for transfers between devices, body(): lax.all_gather(variant_pre, 'dp', axis=0, tiled=True)  35.3 us
  transfers between devices with their start and end apart: 7, of which 7 were waited for; matrix products, arithmetic and copies ran while one was open for 3% of the time, Pallas kernels for 0%

commit v1 on v0

--- a/solution.py
+++ b/solution.py
@@ -3,6 +3,7 @@
 import jax.numpy as jnp
 from jax import lax
 from jax.sharding import PartitionSpec as P
+from jax.lax import psum
 
 
 def gated_values(pre_act, unit_mask):
@@ -50,7 +51,7 @@
     variant_hidden = gated_values(variant_all, unit_mask)
     teacher_part = jnp.dot(parent_all, parent_down, preferred_element_type=jnp.float32)
     student_part = jnp.dot(variant_hidden, local_down, preferred_element_type=jnp.float32)
-    teacher = lax.psum(teacher_part, ("group", "mp"))
+    teacher = psum(psum(teacher_part, "mp"), "group")
     student = lax.psum(student_part, "mp")
     loss_scale = 1.0 / math.sqrt(all_tokens)
     output_grad = ((student - teacher) * loss_scale).astype(jnp.bfloat16)

time: 653 us -> 588 us (0.900)
  waiting for transfers between devices: 590 us -> 526 us
    psum x1, waiting for transfers between devices: 163 us -> 62.3 us  [body(): teacher = psum(psum(teacher_part, 'mp'), 'group')]
    psum x1, waiting for transfers between devices: 93 us -> 127 us  [body(): student = lax.psum(student_part, 'mp')]
where the time goes in v1:
time: 588 us; the launch traced here: 587 us
  waiting for transfers between devices  526 us (89%)
  matrix products  29.7 us (5%)
  between operations  14.8 us (3%)
  other arithmetic  9.67 us (2%)
  local copies, waits for them, and re-layouts  7.1 us (1%)
    psum x1, waiting for transfers between devices, body(): student = lax.psum(student_part, 'mp')  127 us
    psum x1, waiting for transfers between devices, body(): hidden_full = lax.psum(hidden_part, 'dp')  126 us
    reduce_scatter x1, waiting for transfers between devices, body(): lax.psum_scatter(variant_term, 'dp', scatter_dimension=0, tiled=True)  71.3 us
    reduce_scatter x1, waiting for transfers between devices, body(): lax.psum_scatter(parent_term, 'dp', scatter_dimension=0, tiled=True)  66 us
    psum x1, waiting for transfers between devices, body(): teacher = psum(psum(teacher_part, 'mp'), 'group')  62.3 us
    all_gather x1, waiting for transfers between devices, body(): lax.all_gather(parent_hidden, 'dp', axis=0, tiled=True)  37.3 us
    all_gather x1, waiting for transfers between devices, body(): lax.all_gather(variant_pre, 'dp', axis=0, tiled=True)  36 us
  transfers between devices with their start and end apart: 7, of which 7 were waited for; matrix products, arithmetic and copies ran while one was open for 3% of the time, Pallas kernels for 0%

profile of v1, /device:TPU:1, one launch (start us, length us, event | category | flops | bytes accessed | tf_op | source)
XLA Modules:
  0.0 587.2 jit_solution(13210467571178630727)
XLA Ops:
  7.2 1.4 copy-done
  8.7 5.2 fusion.45
  13.9 1.1 copy-done.1
  15.0 5.5 fusion.29
  20.5 0.0 all-gather.5.cloned.1.call-start
  20.6 66.0 %reduce-scatter.5.cloned.1.call-done = f32[48,2,896]{2,0,1:T(8,128)} async-done(((f32[768,2,896]{2,0,1:T(8,128)}), f32[48,2,896]{2,0,1:T(8,128)}) %reduce-scatter.5.cloned.1.call-update) | async-done | bytes 344080 | tf_op jit(solution)/shard_map/reduce_scatter | solution.py:41
  86.6 1.0 convert_element_type.66
  87.6 0.7 fusion.52
  88.4 71.3 %reduce-scatter.3.cloned.1.call-done = f32[48,2,896]{2,0,1:T(8,128)} async-done(((f32[768,2,896]{2,0,1:T(8,128)}), f32[48,2,896]{2,0,1:T(8,128)}) %reduce-scatter.3.cloned.1.call-update) | async-done | bytes 344080 | tf_op jit(solution)/shard_map/reduce_scatter | solution.py:42
  159.6 1.7 convert_element_type.60
  161.3 0.0 all-reduce.9.cloned.1.call-start
  162.1 37.3 %all-gather.5.cloned.1.call-done = bf16[768,896]{1,0:T(8,128)(2,1)} async-done(((bf16[48,896]{1,0:T(8,128)(2,1)}), bf16[768,896]{1,0:T(8,128)(2,1)}) %all-gather.5.cloned.1.call-update) | async-done | bytes 1376272 | tf_op jit(solution)/shard_map/all_gather | solution.py:48
  199.4 3.7 fusion.57
  203.1 36.0 %all-gather.3.cloned.1.call-done = bf16[768,2,896]{2,0,1:T(8,128)(2,1)} async-done(((bf16[48,2,896]{2,0,1:T(8,128)(2,1)}), bf16[768,2,896]{2,0,1:T(8,128)(2,1)}) %all-gather.3.cloned.1.call-update) | async-done | bytes 2752528 | tf_op jit(solution)/shard_map/all_gather | solution.py:49
  239.1 4.0 fusion.31
  243.2 127.0 %all-reduce.9.cloned.1.call-done = (f32[768,512]{1,0:T(8,128)}, f32[768,512]{1,0:T(8,128)}) async-done(((f32[768,512]{1,0:T(8,128)}, f32[768,512]{1,0:T(8,128)}), (f32[768,512]{1,0:T(8,128)}, f32[768,512]{1,0:T(8,128)})) %all-reduce.9.cloned.1.call-update) | async-done | bytes 3145744 | tf_op jit(solution)/shard_map/psum | solution.py:55
  370.2 62.3 %all-reduce.5.cloned.1.call-done = f32[768,512]{1,0:T(8,128)} async-done(((f32[768,512]{1,0:T(8,128)}), f32[768,512]{1,0:T(8,128)}) %all-reduce.5.cloned.1.call-update) | async-done | bytes 1572880 | tf_op jit(solution)/shard_map/psum | solution.py:54
  432.6 2.3 multiply_convert_fusion
  434.9 3.7 fusion.39
  438.6 4.1 convolution_bitcast_fusion
  442.7 125.6 %all-reduce.7.cloned.1.call-done = f32[768,896]{1,0:T(8,128)} async-done(((f32[768,896]{1,0:T(8,128)}), f32[768,896]{1,0:T(8,128)}) %all-reduce.7.cloned.1.call-update) | async-done | bytes 2752528 | tf_op jit(solution)/shard_map/psum | solution.py:64
  568.3 4.0 fusion.36
  572.3 3.4 fusion.26
  575.8 4.6 copy.9
  (17 shorter events, 0.3 us)
Async XLA Ops:
  7.2 1.5 copy-start
  7.2 79.4 %reduce-scatter.5.cloned.1.call-start = ((), (), s32[]{:S(2)}) async-start(), calls=%async_computation.4 | async-start | bytes 5849088 | tf_op jit(solution)/shard_map/reduce_scatter | solution.py:41
  13.9 1.1 copy-start.1
  13.9 145.8 %reduce-scatter.3.cloned.1.call-start = ((), (), s32[]{:S(2)}) async-start(), calls=%async_computation.2 | async-start | bytes 5849088 | tf_op jit(solution)/shard_map/reduce_scatter | solution.py:42
  20.5 178.9 %all-gather.5.cloned.1.call-start = ((), (), s32[]{:S(2)}) async-start(), calls=%async_computation.5 | async-start | bytes 1462272 | tf_op jit(solution)/shard_map/all_gather | solution.py:48
  88.3 150.8 %all-gather.3.cloned.1.call-start = ((), (), s32[]{:S(2)}) async-start(), calls=%async_computation.3 | async-start | bytes 2924544 | tf_op jit(solution)/shard_map/all_gather | solution.py:49
  161.3 208.8 %all-reduce.9.cloned.1.call-start = ((), (), s32[]{:S(2)}) async-start(), calls=%async_computation.8 | async-start | bytes 6291456 | tf_op jit(solution)/shard_map/psum | solution.py:55
  162.0 77.1 %copy-start.2 = (bf16[1,896,512]{2,1,0:T(8,128)(2,1)S(1)}, bf16[1,896,512]{2,1,0:T(8,128)(2,1)}, u32[]{:S(2)}) copy-start(bf16[1,896,512]{2,1,0:T(8,128)(2,1)} %param.10) | copy-start | bytes 2752516
  243.1 189.4 %all-reduce.5.cloned.1.call-start = ((), (), s32[]{:S(2)}) async-start(), calls=%async_computation.6 | async-start | bytes 3145728 | tf_op jit(solution)/shard_map/psum | solution.py:54
  370.2 198.1 %all-reduce.7.cloned.1.call-start = ((), (), s32[]{:S(2)}) async-start(), calls=%async_computation.7 | async-start | bytes 5505024 | tf_op jit(solution)/shard_map/psum | solution.py:64
Sparse Core Ops, SparseCore 0:
  14.0 72.5 reduce-scatter.4
  89.1 70.4 reduce-scatter.2
  162.1 37.2 all-gather.4
  201.6 37.4 all-gather.2
  243.3 126.8 all-reduce.8
  372.4 60.1 all-reduce.4
  438.7 129.5 all-reduce.6
